TPU v7x, 256 devices: a whole 4x4x8 slice. The times are simulated.
256 devices in a mesh: dp: 8 (over z_hi, x), tensor: 8 (over z_lo, core), fsdp: 4 (over y).
Axes of the slice: x: 4, y: 4, z: 8 (z_hi: 2, z_lo: 4; z = z_hi * 4 + z_lo), core: 2. Of those that a mesh axis runs over, the one named last changes fastest.
Arguments:
- train_acts: bfloat16 [8192, 4096], P(('dp', 'fsdp'), 'tensor'), may hold values from -6 to 6
- val_acts: bfloat16 [8192, 4096], P(('dp', 'fsdp'), 'tensor'), may hold values from -6 to 6
- train_cot: bfloat16 [8192, 4096], P(('dp', 'fsdp'), 'tensor'), may hold values from -6 to 6
- val_cot: bfloat16 [8192, 4096], P(('dp', 'fsdp'), 'tensor'), may hold values from -6 to 6
- train_lengths: int32 [128], P(('dp', 'fsdp')), may hold values from 16 to 64
- val_lengths: int32 [128], P(('dp', 'fsdp')), may hold values from 16 to 64
- gate_weight: bfloat16 [4096, 11008], P(('dp', 'fsdp'), 'tensor'), may hold values from -0.09375 to 0.09375
- up_weight: bfloat16 [4096, 11008], P(('dp', 'fsdp'), 'tensor'), may hold values from -0.09375 to 0.09375
- in_basis: bfloat16 [11008, 64], P('tensor'), may hold values from -0.0546875 to 0.0546875
- out_basis: bfloat16 [4096, 128], P('tensor'), may hold values from -0.09375 to 0.09375
Outputs:
- scores: float32 [128, 128], P(('dp', 'fsdp'))
Inputs may be any that keep to these rules, and one draw needn't show every extreme that they name: `train_lengths`: an example's first length slots hold its tokens, the rest are padding. `val_lengths`: as for the training examples.
All inputs are finite; a program needn't handle non-finite values.
Results may differ from a plain program's by a relative error of at most 0.004.
Values may be sent and summed in bfloat16 or wider, within the bound.
A program may use at most 128 MiB of HBM per device.

v0:
```python
import jax
import jax.numpy as jnp
from jax import lax
from jax.sharding import PartitionSpec as P

SEQ = 64


def side_by_side(arrays, axis, dim, along):
    widths = [a.shape[along] for a in arrays]
    both = jnp.concatenate(arrays, axis=along)
    out = lax.all_gather(both, axis, axis=dim, tiled=True)
    return tuple(jnp.split(out, [sum(widths[:k]) for k in range(1, len(widths))], axis=along))


def from_everyone(array, axis):
    copies = jnp.broadcast_to(array, (lax.axis_size(axis), *array.shape))
    return lax.all_to_all(copies, axis, split_axis=0, concat_axis=0, tiled=True)


def taken_together(array, axis):
    return from_everyone(array, axis).sum(axis=0)


def in_blocks(array, dim, count):
    shape = array.shape
    tiles = array.reshape(*shape[:dim], count, shape[dim] // count, *shape[dim + 1 :])
    return jnp.moveaxis(tiles, dim, 0)


def summed_on_arrival(array, axis, dim):
    tiles = in_blocks(array, dim, lax.axis_size(axis))
    arrived = lax.all_to_all(tiles, axis, split_axis=0, concat_axis=0, tiled=True)
    return arrived.sum(axis=0)


def laid_out(tiles, dim):
    shape = list(tiles.shape[1:])
    shape[dim] *= tiles.shape[0]
    return jnp.moveaxis(tiles, 0, dim).reshape(shape)


def gather_directly(array, axis, dim):
    tiles = from_everyone(array, axis)
    return laid_out(tiles, dim)


def outer_sums(in_proj, out_proj, valid):
    in_three = in_proj.reshape(valid.shape[0], valid.shape[1], in_proj.shape[1]) * valid[:, :, None]
    out_three = out_proj.reshape(valid.shape[0], valid.shape[1], out_proj.shape[1])
    return jnp.einsum("esj,esk->ejk", in_three, out_three, precision=lax.Precision.HIGHEST)


def on_device(
    train_acts,
    val_acts,
    train_cot,
    val_cot,
    train_lengths,
    val_lengths,
    gate_weight,
    up_weight,
    in_basis,
    out_basis,
):
    train_full, val_full = side_by_side((train_acts, val_acts), "tensor", 1, 0)
    activations = jnp.concatenate([train_full, val_full], axis=0)
    cotangents = jnp.concatenate([train_cot, val_cot], axis=0)
    pieces = side_by_side((gate_weight, up_weight), ("dp", "fsdp"), 0, 1)
    gate_sum = jnp.dot(activations, pieces[0], preferred_element_type=jnp.float32)
    up_sum = jnp.dot(activations, pieces[1], preferred_element_type=jnp.float32)
    hidden = (jax.nn.silu(gate_sum) * up_sum).astype(jnp.bfloat16)
    in_part = jnp.dot(hidden, in_basis, preferred_element_type=jnp.float32)
    out_part = jnp.dot(cotangents, out_basis, preferred_element_type=jnp.float32)
    lengths = jnp.concatenate([train_lengths, val_lengths], axis=0)
    valid = (jnp.arange(SEQ, dtype=jnp.int32)[None, :] < lengths[:, None]).astype(jnp.float32)
    out_proj = taken_together(out_part, "tensor")
    partial_value = outer_sums(in_part, out_proj, valid)
    shares = summed_on_arrival(partial_value, "tensor", 1)
    sketch = gather_directly(shares, "tensor", 1)
    flat_sketch = sketch.reshape(sketch.shape[0], sketch.shape[1] * sketch.shape[2])
    unit_rows = flat_sketch * lax.rsqrt(
        jnp.sum(flat_sketch * flat_sketch, axis=1, keepdims=True) + 1e-06
    )
    train_count = train_lengths.shape[0]
    train_unit = unit_rows[:train_count]
    val_local = unit_rows[train_count:]
    width_all = flat_sketch.shape[1]
    share = width_all // lax.axis_size("tensor")
    first = lax.axis_index("tensor") * share
    train_share = lax.dynamic_slice_in_dim(train_unit, first, share, 1)
    val_share_local = lax.dynamic_slice_in_dim(val_local, first, share, 1)
    val_share = gather_directly(val_share_local, ("dp", "fsdp"), 0)
    partial_scores = jnp.dot(
        train_share,
        val_share.T,
        precision=lax.Precision.HIGHEST,
        preferred_element_type=jnp.float32,
    )
    product = lax.psum(partial_scores, "tensor")
    return product * jnp.sqrt(jnp.float32(width_all))


def solution(mesh):
    placed = (
        P(("dp", "fsdp"), "tensor"),
        P(("dp", "fsdp"), "tensor"),
        P(("dp", "fsdp"), "tensor"),
        P(("dp", "fsdp"), "tensor"),
        P(("dp", "fsdp")),
        P(("dp", "fsdp")),
        P(("dp", "fsdp"), "tensor"),
        P(("dp", "fsdp"), "tensor"),
        P("tensor", None),
        P("tensor", None),
    )
    return jax.shard_map(
        on_device, mesh=mesh, in_specs=placed, out_specs=P(("dp", "fsdp"), None), check_vma=False
    )
```

profile of v0, /device:TPU:1, one launch (start us, length us, event | category | flops | bytes accessed | tf_op | source)
XLA Modules:
  0.0 658.2 jit_solution(8967258331673198613)
XLA Ops:
  6.5 0.0 all-gather.3.cloned.1.call-start
  6.6 2.0 pad_maximum_fusion.1
  8.6 0.0 all-gather.3.cloned.1.call-update
  8.6 0.0 all-gather.5.cloned.1.call-start
  8.6 2.0 pad_maximum_fusion
  10.6 0.0 all-gather.5.cloned.1.call-update
  10.7 0.3 fusion.13
  11.0 0.0 copy-start.4
  11.0 1.5 broadcast_in_dim.6
  12.5 7.4 %all-to-all-start = ((f32[8,512,128]{2,1,0:T(8,128)}), f32[8,512,128]{2,1,0:T(8,128)S(1)}, u32[]{:S(2)}, u32[]{:S(2)}) async-start(f32[8,512,128]{2,1,0:T(8,128)} %broadcast_in_dim.6), calls=%async_computation | async-start | bytes 4194304 | tf_op jit(solution)/shard_map/all_to_all | solution.py:18
  19.9 0.1 pad_add_fusion
  19.9 0.1 fusion.20
  20.0 77.4 %all-to-all-done = f32[8,512,128]{2,1,0:T(8,128)S(1)} async-done(((f32[8,512,128]{2,1,0:T(8,128)}), f32[8,512,128]{2,1,0:T(8,128)S(1)}, u32[]{:S(2)}, u32[]{:S(2)}) %all-to-all-start) | async-done | bytes 2097184 | tf_op jit(solution)/shard_map/all_to_all | solution.py:18
  97.4 0.1 reduce_sum.27
  97.5 9.1 %all-gather.3.cloned.1.call-done = bf16[512,4096]{1,0:T(8,128)(2,1)} async-done(((bf16[512,512]{1,0:T(8,128)(2,1)}), bf16[512,4096]{1,0:T(8,128)(2,1)}) %all-gather.3.cloned.1.call-update) | async-done | bytes 4194320 | tf_op jit(solution)/shard_map/all_gather | solution.py:12
  106.6 453.0 %all-gather.5.cloned.1.call-done = bf16[4096,2752]{0,1:T(8,128)(2,1)} async-done(((bf16[128,2752]{0,1:T(8,128)(2,1)}), bf16[4096,2752]{0,1:T(8,128)(2,1)}) %all-gather.5.cloned.1.call-update) | async-done | bytes 22544400 | tf_op jit(solution)/shard_map/all_gather | solution.py:12
  559.7 11.2 %fusion.2 = f32[512,1376]{0,1:T(8,128)} fusion(bf16[512,4096]{1,0:T(8,128)(2,1)} %all-gather.3.cloned.1.call-done, bf16[4096,2752]{0,1:T(8,128)(2,1)} %all-gather.5.cloned.1.call-done), kind=kOutput, calls=%fused_computation.2 | convolution fusion | flops 5771362304 | bytes 18284544 | tf_op jit(solution)/shard_map/dot_general | solution.py:70
  570.9 12.9 %fusion.11 = f32[512,64]{0,1:T(8,128)S(1)} fusion(bf16[1376,64]{0,1:T(8,128)(2,1)S(1)} %copy-done, bf16[512,4096]{1,0:T(8,128)(2,1)} %all-gather.3.cloned.1.call-done, bf16[4096,2752]{0,1:T(8,128)(2,1)} %all-gather.5.cloned.1.call-done, f32[512,1376]{0,1:T(8,128)} %fusion.2), kind=kOutput, calls=%fused_computation.6 | convolution fusion | flops 5865766912 | bytes 18591744 | tf_op jit(solution)/shard_map/dot_general | solution.py:73
  583.8 0.1 reshape.40
  583.9 0.4 convolution_bitcast_fusion
  584.3 13.1 %all_to_all.20 = f32[8,8,8,128]{3,2,1,0:T(8,128)S(1)} all-to-all(f32[8,8,8,128]{3,2,1,0:T(8,128)S(1)} %bitcast.24), channel_id=1, replica_groups=mesh['dp'=8,'tensor'=8,'fsdp'=4] {'tensor'}, dimensions={0} | all-to-all | bytes 524288 | tf_op jit(solution)/shard_map/all_to_all | solution.py:33
  597.5 0.7 broadcast_in_dim.14
  598.2 4.4 all-to-all-start.2
  602.6 8.7 %all-to-all-done.2 = f32[8,8,8,128]{3,2,1,0:T(8,128)S(1)} async-done(((f32[8,8,8,128]{3,2,1,0:T(8,128)}), f32[8,8,8,128]{3,2,1,0:T(8,128)S(1)}, u32[]{:S(2)}, u32[]{:S(2)}) %all-to-all-start.2) | async-done | bytes 262176 | tf_op jit(solution)/shard_map/all_to_all | solution.py:18
  611.3 0.2 multiply_reduce_fusion
  611.4 0.2 bitcast_multiply_fusion
  611.7 0.1 broadcast_in_dim.15
  611.8 22.4 %all_to_all.21 = f32[32,4,1024]{2,1,0:T(4,128)S(1)} all-to-all(f32[32,4,1024]{2,1,0:T(4,128)S(1)} %broadcast_in_dim.15), channel_id=1, replica_groups=mesh['dp'=8,'tensor'=8,'fsdp'=4] {'dp','fsdp'}, dimensions={0} | all-to-all | bytes 1048576 | tf_op jit(solution)/shard_map/all_to_all | solution.py:18
  634.2 0.2 reshape.43
  634.3 0.5 fusion.18
  634.9 15.9 %psum.7 = f32[4,128]{1,0:T(4,128)S(1)} all-reduce(f32[4,128]{1,0:T(4,128)S(1)} %fusion.18), channel_id=1, replica_groups=mesh['dp'=8,'tensor'=8,'fsdp'=4] {'tensor'}, use_global_device_ids=true, to_apply=%region_3.4 | all-reduce | flops 512 | bytes 4096 | tf_op jit(solution)/shard_map/psum | solution.py:100
  650.8 0.6 broadcast_multiply_fusion
  (17 shorter events, 0.1 us)
Async XLA Ops:
  6.5 564.3 %copy-start = (bf16[1376,64]{0,1:T(8,128)(2,1)S(1)}, bf16[1376,64]{0,1:T(8,128)(2,1)}, u32[]{:S(2)}) copy-start(bf16[1376,64]{0,1:T(8,128)(2,1)} %param.18) | copy-start | bytes 528388
  6.5 4.1 copy-start.2
  6.5 4.1 copy-start.1
  6.5 4.1 copy-start.3
  6.5 100.1 %all-gather.3.cloned.1.call-start = ((), (), s32[]{:S(2)}) async-start(), calls=%async_computation.4 | async-start | bytes 4718592 | tf_op jit(solution)/shard_map/all_gather | solution.py:12
  8.6 551.1 %all-gather.5.cloned.1.call-start = ((), (), s32[]{:S(2)}) async-start(), calls=%async_computation.5 | async-start | bytes 23248896 | tf_op jit(solution)/shard_map/all_gather | solution.py:12
  11.0 8.9 %copy-start.4 = (s32[4]{0:T(128)S(1)}, s32[4]{0:T(128)}, u32[]{:S(2)}) copy-start(s32[4]{0:T(128)} %param.15) | copy-start | bytes 52
  11.0 8.9 %copy-start.5 = (s32[4]{0:T(128)S(1)}, s32[4]{0:T(128)}, u32[]{:S(2)}) copy-start(s32[4]{0:T(128)} %param.14) | copy-start | bytes 52
  12.5 84.9 %all-to-all-start = ((f32[8,512,128]{2,1,0:T(8,128)}), f32[8,512,128]{2,1,0:T(8,128)S(1)}, u32[]{:S(2)}, u32[]{:S(2)}) async-start(f32[8,512,128]{2,1,0:T(8,128)} %broadcast_in_dim.6), calls=%async_computation | async-start | bytes 4194304 | tf_op jit(solution)/shard_map/all_to_all | solution.py:18
  598.2 13.1 %all-to-all-start.2 = ((f32[8,8,8,128]{3,2,1,0:T(8,128)}), f32[8,8,8,128]{3,2,1,0:T(8,128)S(1)}, u32[]{:S(2)}, u32[]{:S(2)}) async-start(f32[8,8,8,128]{3,2,1,0:T(8,128)} %broadcast_in_dim.14), calls=%async_computation.2 | async-start | bytes 524288 | tf_op jit(solution)/shard_map/all_to_all | solution.py:18
Sparse Core Ops, SparseCore 0:
  9.1 97.4 all-gather.2
  109.8 449.7 all-gather.4
where the time goes:
time: 659 us; the launch traced here: 658 us
  waiting for transfers between devices  548 us (83%)
  blocking collectives  51.4 us (8%)
  matrix products  25.3 us (4%)
  between operations  13.5 us (2%)
  starting transfers between devices  11.8 us (2%)
    all_gather x2, waiting for transfers between devices, side_by_side(): out = lax.all_gather(both, axis, axis=dim, tiled=True)  462 us
    all_to_all x2, waiting for transfers between devices, from_everyone(): return lax.all_to_all(copies, axis, split_axis=0, concat_axis=0, tiled=True)  86.1 us
    all_to_all x1, blocking collectives, from_everyone(): return lax.all_to_all(copies, axis, split_axis=0, concat_axis=0, tiled=True)  22.4 us
    psum x1, blocking collectives, on_device(): product = lax.psum(partial_scores, 'tensor')  15.9 us
  transfers between devices with their start and end apart: 4, of which 4 were waited for; matrix products, arithmetic and copies ran while one was open for 1% of the time, Pallas kernels for 0%

commit v1 on v0

--- a/solution.py
+++ b/solution.py
@@ -97,7 +97,7 @@
         precision=lax.Precision.HIGHEST,
         preferred_element_type=jnp.float32,
     )
-    product = lax.psum(partial_scores, "tensor")
+    product = jnp.sum(lax.all_gather(partial_scores, "tensor"), axis=0)
     return product * jnp.sqrt(jnp.float32(width_all))
 
 

time: 659 us -> 658 us (level)
    psum x1 -> x0, blocking collectives: 15.9 us -> none  [on_device(): product = lax.psum(partial_scores, 'tensor')]
    all_gather x0 -> x1, blocking collectives: none -> 15.5 us  [on_device(): product = jnp.sum(lax.all_gather(partial_scores, 'tensor'), axis=0)]
where the time goes in v1:
time: 658 us
  waiting for transfers between devices  548 us (83%)
  blocking collectives  51 us (8%)
  matrix products  25.3 us (4%)
  between operations  13.5 us (2%)
  starting transfers between devices  11.8 us (2%)
    all_gather x2, waiting for transfers between devices, side_by_side(): out = lax.all_gather(both, axis, axis=dim, tiled=True)  462 us
    all_to_all x2, waiting for transfers between devices, from_everyone(): return lax.all_to_all(copies, axis, split_axis=0, concat_axis=0, tiled=True)  86.1 us
    all_to_all x1, blocking collectives, from_everyone(): return lax.all_to_all(copies, axis, split_axis=0, concat_axis=0, tiled=True)  22.4 us
    all_gather x1, blocking collectives, on_device(): product = jnp.sum(lax.all_gather(partial_scores, 'tensor'), axis=0)  15.5 us
  transfers between devices with their start and end apart: 4, of which 4 were waited for; matrix products, arithmetic and copies ran while one was open for 1% of the time, Pallas kernels for 0%

profile of v1, /device:TPU:1, one launch (start us, length us, event | category | flops | bytes accessed | tf_op | source)
XLA Modules:
  0.0 657.8 jit_solution(813282748647787219)
XLA Ops:
  6.5 0.0 all-gather.5.cloned.1.call-start
  6.6 2.0 pad_maximum_fusion.1
  8.6 0.0 all-gather.5.cloned.1.call-update
  8.6 0.0 all-gather.7.cloned.1.call-start
  8.6 2.0 pad_maximum_fusion
  10.6 0.0 all-gather.7.cloned.1.call-update
  10.7 0.3 fusion.13
  11.0 0.0 copy-start.4
  11.0 1.5 broadcast_in_dim.6
  12.5 7.4 %all-to-all-start = ((f32[8,512,128]{2,1,0:T(8,128)}), f32[8,512,128]{2,1,0:T(8,128)S(1)}, u32[]{:S(2)}, u32[]{:S(2)}) async-start(f32[8,512,128]{2,1,0:T(8,128)} %broadcast_in_dim.6), calls=%async_computation | async-start | bytes 4194304 | tf_op jit(solution)/shard_map/all_to_all | solution.py:18
  19.9 0.1 pad_add_fusion
  19.9 0.1 fusion.19
  20.0 77.4 %all-to-all-done = f32[8,512,128]{2,1,0:T(8,128)S(1)} async-done(((f32[8,512,128]{2,1,0:T(8,128)}), f32[8,512,128]{2,1,0:T(8,128)S(1)}, u32[]{:S(2)}, u32[]{:S(2)}) %all-to-all-start) | async-done | bytes 2097184 | tf_op jit(solution)/shard_map/all_to_all | solution.py:18
  97.4 0.1 reduce_sum.36
  97.5 9.1 %all-gather.5.cloned.1.call-done = bf16[512,4096]{1,0:T(8,128)(2,1)} async-done(((bf16[512,512]{1,0:T(8,128)(2,1)}), bf16[512,4096]{1,0:T(8,128)(2,1)}) %all-gather.5.cloned.1.call-update) | async-done | bytes 4194320 | tf_op jit(solution)/shard_map/all_gather | solution.py:12
  106.6 453.0 %all-gather.7.cloned.1.call-done = bf16[4096,2752]{0,1:T(8,128)(2,1)} async-done(((bf16[128,2752]{0,1:T(8,128)(2,1)}), bf16[4096,2752]{0,1:T(8,128)(2,1)}) %all-gather.7.cloned.1.call-update) | async-done | bytes 22544400 | tf_op jit(solution)/shard_map/all_gather | solution.py:12
  559.7 11.2 %fusion.2 = f32[512,1376]{0,1:T(8,128)} fusion(bf16[512,4096]{1,0:T(8,128)(2,1)} %all-gather.5.cloned.1.call-done, bf16[4096,2752]{0,1:T(8,128)(2,1)} %all-gather.7.cloned.1.call-done), kind=kOutput, calls=%fused_computation.2 | convolution fusion | flops 5771362304 | bytes 18284544 | tf_op jit(solution)/shard_map/dot_general | solution.py:70
  570.9 12.9 %fusion.11 = f32[512,64]{0,1:T(8,128)S(1)} fusion(bf16[1376,64]{0,1:T(8,128)(2,1)S(1)} %copy-done, bf16[512,4096]{1,0:T(8,128)(2,1)} %all-gather.5.cloned.1.call-done, bf16[4096,2752]{0,1:T(8,128)(2,1)} %all-gather.7.cloned.1.call-done, f32[512,1376]{0,1:T(8,128)} %fusion.2), kind=kOutput, calls=%fused_computation.6 | convolution fusion | flops 5865766912 | bytes 18591744 | tf_op jit(solution)/shard_map/dot_general | solution.py:73
  583.8 0.1 reshape.40
  583.9 0.4 convolution_bitcast_fusion
  584.3 13.1 %all_to_all.20 = f32[8,8,8,128]{3,2,1,0:T(8,128)S(1)} all-to-all(f32[8,8,8,128]{3,2,1,0:T(8,128)S(1)} %bitcast.26), channel_id=1, replica_groups=mesh['dp'=8,'tensor'=8,'fsdp'=4] {'tensor'}, dimensions={0} | all-to-all | bytes 524288 | tf_op jit(solution)/shard_map/all_to_all | solution.py:33
  597.5 0.7 broadcast_in_dim.14
  598.2 4.4 all-to-all-start.2
  602.6 8.7 %all-to-all-done.2 = f32[8,8,8,128]{3,2,1,0:T(8,128)S(1)} async-done(((f32[8,8,8,128]{3,2,1,0:T(8,128)}), f32[8,8,8,128]{3,2,1,0:T(8,128)S(1)}, u32[]{:S(2)}, u32[]{:S(2)}) %all-to-all-start.2) | async-done | bytes 262176 | tf_op jit(solution)/shard_map/all_to_all | solution.py:18
  611.3 0.2 multiply_reduce_fusion
  611.4 0.2 bitcast_multiply_fusion
  611.7 0.1 broadcast_in_dim.15
  611.8 22.4 %all_to_all.21 = f32[32,4,1024]{2,1,0:T(4,128)S(1)} all-to-all(f32[32,4,1024]{2,1,0:T(4,128)S(1)} %broadcast_in_dim.15), channel_id=1, replica_groups=mesh['dp'=8,'tensor'=8,'fsdp'=4] {'dp','fsdp'}, dimensions={0} | all-to-all | bytes 1048576 | tf_op jit(solution)/shard_map/all_to_all | solution.py:18
  634.2 0.2 reshape.43
  634.3 0.5 convolution_bitcast_fusion.1
  634.9 15.5 %all-gather.1 = f32[8,4,128]{2,1,0:T(4,128)S(1)} all-gather(f32[1,4,128]{2,1,0:T(4,128)S(1)} %convolution_bitcast_fusion.1), channel_id=2, replica_groups=mesh['dp'=8,'tensor'=8,'fsdp'=4] {'tensor'}, dimensions={0}, use_global_device_ids=true | all-gather | bytes 18432 | tf_op jit(solution)/shard_map/all_gather | solution.py:100
  650.4 0.6 broadcast_multiply_fusion
  (18 shorter events, 0.2 us)
Async XLA Ops:
  6.5 564.3 %copy-start = (bf16[1376,64]{0,1:T(8,128)(2,1)S(1)}, bf16[1376,64]{0,1:T(8,128)(2,1)}, u32[]{:S(2)}) copy-start(bf16[1376,64]{0,1:T(8,128)(2,1)} %param.18) | copy-start | bytes 528388
  6.5 4.1 copy-start.2
  6.5 4.1 copy-start.1
  6.5 4.1 copy-start.3
  6.5 100.1 %all-gather.5.cloned.1.call-start = ((), (), s32[]{:S(2)}) async-start(), calls=%async_computation.4 | async-start | bytes 4718592 | tf_op jit(solution)/shard_map/all_gather | solution.py:12
  8.6 551.1 %all-gather.7.cloned.1.call-start = ((), (), s32[]{:S(2)}) async-start(), calls=%async_computation.5 | async-start | bytes 23248896 | tf_op jit(solution)/shard_map/all_gather | solution.py:12
  11.0 8.9 %copy-start.4 = (s32[4]{0:T(128)S(1)}, s32[4]{0:T(128)}, u32[]{:S(2)}) copy-start(s32[4]{0:T(128)} %param.15) | copy-start | bytes 52
  11.0 8.9 %copy-start.5 = (s32[4]{0:T(128)S(1)}, s32[4]{0:T(128)}, u32[]{:S(2)}) copy-start(s32[4]{0:T(128)} %param.14) | copy-start | bytes 52
  12.5 84.9 %all-to-all-start = ((f32[8,512,128]{2,1,0:T(8,128)}), f32[8,512,128]{2,1,0:T(8,128)S(1)}, u32[]{:S(2)}, u32[]{:S(2)}) async-start(f32[8,512,128]{2,1,0:T(8,128)} %broadcast_in_dim.6), calls=%async_computation | async-start | bytes 4194304 | tf_op jit(solution)/shard_map/all_to_all | solution.py:18
  598.2 13.1 %all-to-all-start.2 = ((f32[8,8,8,128]{3,2,1,0:T(8,128)}), f32[8,8,8,128]{3,2,1,0:T(8,128)S(1)}, u32[]{:S(2)}, u32[]{:S(2)}) async-start(f32[8,8,8,128]{3,2,1,0:T(8,128)} %broadcast_in_dim.14), calls=%async_computation.2 | async-start | bytes 524288 | tf_op jit(solution)/shard_map/all_to_all | solution.py:18
Sparse Core Ops, SparseCore 0:
  9.1 97.4 all-gather.4
  109.8 449.7 all-gather.6
